TPU v7x, 32 devices: a whole 2x2x4 slice. The times are simulated.
32 devices in a mesh: patch: 16 (over z, y, core), band: 2 (over x).
Axes of the slice: x: 2, y: 2, z: 4, core: 2. Of those that a mesh axis runs over, the one named last changes fastest.
Arguments:
- latents: float32 [10240, 512], P('patch', 'band'), may hold values from -6 to 6
- edge_latents: float32 [81920, 512], P(('patch', 'band')), may hold values from -6 to 6
- edge_sender: int32 [81920], P(('patch', 'band')), may hold values from 0 to 575, as said below
- edge_receiver: int32 [81920], P(('patch', 'band')), may hold values from 0 to 319
- block_counts: int32 [640], P(('patch', 'band')), may hold values from 16 to 128, as said below
- send_rows: int32 [32, 32, 8], P(('patch', 'band')), may hold values from 0 to 319
- edge_first_weight: bfloat16 [2, 1536, 512], replicated, may hold values from -0.15625 to 0.15625
- edge_first_bias: float32 [2, 512], replicated, may hold values from -3 to 3
- edge_second_weight: bfloat16 [2, 512, 512], replicated
- edge_gain: float32 [2, 512], replicated, may hold values from 0.1 to 1.9
- edge_offset: float32 [2, 512], replicated, may hold values from -3 to 3
- node_first_weight: bfloat16 [2, 1024, 512], replicated, may hold values from -0.1875 to 0.1875
- node_first_bias: float32 [2, 512], replicated, may hold values from -3 to 3
- node_second_weight: bfloat16 [2, 512, 512], replicated
- node_gain: float32 [2, 512], replicated, may hold values from 0.1 to 1.9
- node_offset: float32 [2, 512], replicated, may hold values from -3 to 3
Outputs:
- new_nodes: float32 [10240, 512], P(('patch', 'band'))
- new_edges: float32 [81920, 512], P(('patch', 'band'))
Inputs may be any that keep to these rules, and one draw needn't show every extreme that they name: `edge_sender`: an entry below 320 names a node row of the edge's own device; an entry k above names slot (k - 320) % 8 of the rows that device (k - 320) // 8 sends to the edge's device. `block_counts`: the used slots of a block are its first ones; every device has a full block. send_rows[d, q] lists node rows of device d, numbered within d, that device q receives from d.
All inputs are finite; a program needn't handle non-finite values.
Results may differ from a plain program's by a relative error of at most 0.0045.
Values may be sent and summed in bfloat16 or wider, within the bound.
A program may use at most 128 MiB of HBM per device.

v0:
```python
import functools

import jax
import jax.numpy as jnp
from jax import lax
from jax.experimental import pallas as pl
from jax.experimental.pallas import tpu as pltpu
from jax.sharding import PartitionSpec as P

epsilon = 1e-05
MESH = pl.DeviceIdType.MESH
F32 = jnp.float32
BF16 = jnp.bfloat16


def dot(a, b):
    return jnp.dot(a, b, preferred_element_type=F32)


def layer_norm(values, gain, offset):
    centre = values - jnp.mean(values, axis=-1, keepdims=True)
    spread = jnp.mean(centre * centre, axis=-1, keepdims=True)
    return centre * lax.rsqrt(spread + epsilon) * gain + offset


def swish(v):
    return (v * jax.nn.sigmoid(v)).astype(BF16)


LANES = 128


def hot_columns(conditions, width):
    places = lax.broadcasted_iota(jnp.int32, (conditions[0].shape[0], LANES), 1)
    pieces = []
    for first in range(0, width, LANES):
        hit = places == conditions[0] - first
        for other in conditions[1:]:
            hit = hit | (places == other - first)
        pieces.append(jnp.where(hit, 1.0, 0.0))
    return jnp.concatenate(pieces, axis=1).astype(BF16)


def one_hot_rows(row, height):
    places = lax.broadcasted_iota(jnp.int32, (height, row.shape[1]), 0)
    return jnp.where(places == row, 1.0, 0.0).astype(BF16)


def hot_columns_of(rows, width, step):
    row_place = lax.broadcasted_iota(jnp.int32, (rows, width), 0)
    column_place = lax.broadcasted_iota(jnp.int32, (rows, width), 1)
    return jnp.where(lax.div(row_place, step) == column_place, 1.0, 0.0).astype(BF16)


def to_columns(row):
    return jnp.broadcast_to(row, (row.shape[1], row.shape[1])).T


def used_row(row, count):
    places = lax.broadcasted_iota(jnp.int32, row.shape, 1)
    return jnp.where(places < count, row, -1)


def local_hot(sender, receiver, nodes):
    return hot_columns((jnp.where(sender < nodes, sender, -1), receiver + nodes), 2 * nodes)


def finish_edges(pre, state, sender, row, counts, halo_table, second, gain, offset, nodes):
    pre = pre + dot(hot_columns((sender - nodes,), halo_table.shape[0]), halo_table)
    update = layer_norm(dot(swish(pre), second), gain, offset)
    places = lax.broadcasted_iota(jnp.int32, (LANES, update.shape[1]), 0)
    kept = [
        jnp.where(places < count, update[i * LANES : (i + 1) * LANES], 0.0)
        for i, count in enumerate(counts)
    ]
    state = state + jnp.concatenate(kept, axis=0)
    return state, dot(one_hot_rows(row, nodes), state.astype(BF16))


def node_update(node_low, summed, first, first_bias, second, gain, offset):
    width = node_low.shape[1]
    v = dot(node_low, first[0:width]) + dot(summed.astype(BF16), first[width:]) + first_bias
    return layer_norm(dot(swish(v), second), gain, offset)


def first_kernel(
    patches, bands, chunk,
    counts_ref,
    lat_hbm, senders_hbm, receivers_hbm, lists_hbm, eb_hbm, eg_hbm, eo_hbm, nb_hbm, ng_hbm, no_hbm,
    edge_hbm, ew1_hbm, ew2_hbm, nw1_hbm, nw2_hbm,
    node_hbm, table_hbm, state_hbm, pre_hbm,
    lat_ref, senders_ref, receivers_ref, lists_ref, eb_ref, eg_ref, eo_ref, nb_ref, ng_ref, no_ref,
    node_out, table_out, sender_cols, receiver_cols, rows_ref,
    state, pre, w1, w2, v1, v2, x1, low_out, low_in, wide_in, out_a, out_b, in_a, in_b, table, summed,
    load_sem, store_sem, low_send, low_recv, wide_send, wide_recv, send_a, recv_a, send_b, recv_b,
):
    shards = patches * bands
    patch, band = lax.axis_index("patch"), lax.axis_index("band")
    me = patch * bands + band
    nodes = node_out.shape[0]
    edges, width = state.shape
    chunks = edges // chunk
    blocks = chunk // LANES
    slot = out_a.shape[1]

    loads = [
        pltpu.make_async_copy(src, dst, load_sem.at[i])
        for i, (src, dst) in enumerate((
            (edge_hbm, state), (ew1_hbm.at[0], w1), (ew2_hbm.at[0], w2),
            (nw1_hbm.at[0], v1), (nw2_hbm.at[0], v2), (ew1_hbm.at[1], x1),
            (lat_hbm, lat_ref), (senders_hbm, senders_ref), (receivers_hbm, receivers_ref),
            (lists_hbm.at[0], lists_ref), (eb_hbm, eb_ref), (eg_hbm, eg_ref), (eo_hbm, eo_ref),
            (nb_hbm, nb_ref), (ng_hbm, ng_ref), (no_hbm, no_ref),
        ))
    ]
    for load in [loads[i] for i in (6, 7, 8, 9, 10, 1, 0, 2, 3, 4, 5, 11, 12, 13, 14, 15)]:
        load.start()

    def place(q):
        return (lax.div(q, bands), lax.rem(q, bands))

    barrier = pltpu.get_barrier_semaphore()

    def greet(i, c):
        pl.semaphore_signal(barrier, inc=1, device_id=place(lax.rem(me + i, shards)), device_id_type=MESH)
        return c

    lax.fori_loop(1, shards, greet, 0)
    loads[6].wait()
    low_out[...] = lat_ref[...].astype(BF16)
    mine = pl.ds(pl.multiple_of(band * nodes, nodes), nodes)
    low_in[band] = lat_ref[mine, :].astype(BF16)
    wide_in[band] = lat_ref[mine, :]
    pl.semaphore_wait(barrier, shards - 1)

    exchanges = []
    for src, dst, ss, rs in ((low_out, low_in, low_send, low_recv), (lat_ref, wide_in, wide_send, wide_recv)):
        group = []
        for i in range(1, bands):
            other = lax.rem(band + i, bands)
            copy = pltpu.make_async_remote_copy(
                src_ref=src.at[pl.ds(pl.multiple_of(other * nodes, nodes), nodes)],
                dst_ref=dst.at[band],
                send_sem=ss.at[i],
                recv_sem=rs.at[i],
                device_id=(patch, other),
                device_id_type=MESH,
            )
            copy.start()
            group.append(copy)
        exchanges.append(group)

    def part(c):
        return pl.ds(pl.multiple_of(c * chunk, chunk), chunk)

    for load in loads[7:11]:
        load.wait()

    def turn(j, carry):
        here = pl.ds(pl.multiple_of(j * LANES, LANES), LANES)
        sender_cols[here, :] = to_columns(senders_ref[j])
        receiver_cols[here, :] = to_columns(receivers_ref[j])
        rows_ref[j] = used_row(receivers_ref[j], counts_ref[j])
        return carry

    lax.fori_loop(0, edges // LANES, turn, 0)
    lists = lists_ref[...]
    slots = lists.shape[1]
    spread = hot_columns_of(shards * slots, shards, slots)
    high = dot(spread, jnp.right_shift(lists, 4).astype(F32).astype(BF16))
    picked_all = high * 16.0 + dot(spread, jnp.bitwise_and(lists, 15).astype(F32).astype(BF16))
    row_place = lax.broadcasted_iota(jnp.int32, picked_all.shape, 0)
    slot_place = lax.broadcasted_iota(jnp.int32, picked_all.shape, 1)
    wanted = jnp.sum(
        jnp.where(lax.rem(row_place, slots) == slot_place, picked_all, 0.0), axis=1, keepdims=True
    )
    node_place = lax.broadcasted_iota(jnp.int32, (shards * slots, nodes), 1).astype(F32)
    hot_lists = jnp.where(node_place == wanted, 1.0, 0.0).astype(BF16)
    loads[1].wait()
    loads[0].wait()

    def own_edges(c, carry):
        pre[part(c), :] = dot(state[part(c), :].astype(BF16), w1[0:width, :]) + eb_ref[0:1, :]
        return carry

    lax.fori_loop(0, chunks, own_edges, 0)

    for copy in exchanges[0]:
        copy.wait()
    node_low = jnp.concatenate([low_in[i] for i in range(bands)], axis=1)

    def transfer(i, out, inn, ss, rs):
        q = lax.rem(me + i, shards)
        return pltpu.make_async_remote_copy(
            src_ref=out.at[q],
            dst_ref=inn.at[me],
            send_sem=ss.at[i],
            recv_sem=rs.at[i],
            device_id=place(q),
            device_id_type=MESH,
        )

    def send_halo(node_low, out, inn, ss, rs):
        picked = dot(hot_lists, node_low)
        out[...] = picked.reshape(shards, slot, width).astype(BF16)
        inn[me] = out[me]

        def go(i, c):
            transfer(i, out, inn, ss, rs).start()
            return c

        lax.fori_loop(1, shards, go, 0)

    def await_halo(out, inn, ss, rs):
        def stop(i, c):
            transfer(i, out, inn, ss, rs).wait()
            return c

        lax.fori_loop(1, shards, stop, 0)
        return inn[...].astype(F32).reshape(shards * slot, width).astype(BF16)

    send_halo(node_low, out_a, in_a, send_a, recv_a)
    table[0:nodes, :] = dot(node_low, w1[width : 2 * width, :]).astype(BF16)
    table[nodes:, :] = dot(node_low, w1[2 * width :, :]).astype(BF16)

    def own_nodes(c, carry):
        pre[part(c), :] += dot(local_hot(sender_cols[part(c), :], receiver_cols[part(c), :], nodes), table[...])
        return carry

    lax.fori_loop(0, chunks, own_nodes, 0)
    for load in loads[2:6] + loads[11:]:
        load.wait()
    halo = await_halo(out_a, in_a, send_a, recv_a)
    table_out[...] = dot(halo, w1[width : 2 * width, :]).astype(BF16)
    summed[...] = jnp.zeros_like(summed)

    def finish(c, carry):
        fresh, added = finish_edges(
            pre[part(c), :], state[part(c), :], sender_cols[part(c), :],
            jnp.concatenate([rows_ref[c * blocks + i] for i in range(blocks)], axis=1),
            [counts_ref[c * blocks + i] for i in range(blocks)], table_out[...],
            w2[...], eg_ref[0:1, :], eo_ref[0:1, :], nodes,
        )
        state[part(c), :] = fresh
        summed[...] += added
        return carry

    lax.fori_loop(0, chunks, finish, 0)
    for copy in exchanges[1]:
        copy.wait()
    node_state = jnp.concatenate([wide_in[i] for i in range(bands)], axis=1) + node_update(
        node_low, summed[...], v1, nb_ref[0:1, :], v2[...], ng_ref[0:1, :], no_ref[0:1, :]
    )
    node_out[...] = node_state
    save_nodes = pltpu.make_async_copy(node_out, node_hbm, store_sem.at[2])
    save_nodes.start()
    node_low = node_state.astype(BF16)
    send_halo(node_low, out_b, in_b, send_b, recv_b)
    save_state = pltpu.make_async_copy(state, state_hbm, store_sem.at[0])
    save_state.start()
    table[0:nodes, :] = dot(node_low, x1[width : 2 * width, :]).astype(BF16)
    table[nodes:, :] = dot(node_low, x1[2 * width :, :]).astype(BF16)

    def begin(c, carry):
        pre[part(c), :] = (
            dot(state[part(c), :].astype(BF16), x1[0:width, :])
            + eb_ref[1:2, :]
            + dot(local_hot(sender_cols[part(c), :], receiver_cols[part(c), :], nodes), table[...])
        )
        return carry

    lax.fori_loop(0, chunks, begin, 0)
    save_pre = pltpu.make_async_copy(pre, pre_hbm, store_sem.at[1])
    save_pre.start()
    halo = await_halo(out_b, in_b, send_b, recv_b)
    table_out[...] = dot(halo, x1[width : 2 * width, :]).astype(BF16)
    save_table = pltpu.make_async_copy(table_out, table_hbm, store_sem.at[3])
    save_table.start()
    for save in (save_nodes, save_state, save_pre, save_table):
        save.wait()


def second_kernel(
    chunks,
    counts_ref, pre_ref, state_ref, senders_ref, receivers_ref, table_ref, ew2_ref, eg_ref, eo_ref,
    node_ref, nw1_ref, nb_ref, nw2_ref, ng_ref, no_ref,
    nodes_out, edges_out,
    summed,
):
    step = pl.program_id(0)
    nodes = node_ref.shape[0]

    @pl.when(step == 0)
    def _():
        summed[...] = jnp.zeros_like(summed)

    blocks = senders_ref.shape[0]
    counts = [counts_ref[step * blocks + i] for i in range(blocks)]
    fresh, added = finish_edges(
        pre_ref[...], state_ref[...],
        jnp.concatenate([to_columns(senders_ref[i]) for i in range(blocks)], axis=0),
        jnp.concatenate([used_row(receivers_ref[i], counts[i]) for i in range(blocks)], axis=1),
        counts, table_ref[...],
        ew2_ref[0], eg_ref[1:2, :], eo_ref[1:2, :], nodes,
    )
    edges_out[...] = fresh
    summed[...] += added

    @pl.when(step == chunks - 1)
    def _():
        old = node_ref[...]
        nodes_out[...] = old + node_update(
            old.astype(BF16), summed[...], nw1_ref.at[0], nb_ref[1:2, :], nw2_ref[0], ng_ref[1:2, :], no_ref[1:2, :]
        )


def shards_body(
    patches, bands,
    latents, edge_latents, edge_sender, edge_receiver, block_counts, send_rows,
    edge_first_weight, edge_first_bias, edge_second_weight, edge_gain, edge_offset,
    node_first_weight, node_first_bias, node_second_weight, node_gain, node_offset,
):
    shards = patches * bands
    edges, width = edge_latents.shape
    block = edges // block_counts.shape[0]
    nodes = latents.shape[0] // bands
    slot = send_rows.shape[2]
    chunk = next(c for c in (512, 256, 128) if edges % c == 0 and block == LANES)
    chunks = edges // chunk
    senders = edge_sender.reshape(edges // LANES, 1, LANES)
    receivers = edge_receiver.reshape(edges // LANES, 1, LANES)
    scalars, anywhere = pl.BlockSpec(memory_space=pltpu.SMEM), pl.BlockSpec(memory_space=pl.ANY)
    dma = pltpu.SemaphoreType.DMA
    half = latents.shape[1]
    node_state, table, state, pre = pl.pallas_call(
        functools.partial(first_kernel, patches, bands, chunk),
        out_shape=(
            jax.ShapeDtypeStruct((nodes, width), F32),
            jax.ShapeDtypeStruct((shards * slot, width), BF16),
            jax.ShapeDtypeStruct((edges, width), F32),
            jax.ShapeDtypeStruct((edges, width), F32),
        ),
        in_specs=[scalars] + [anywhere] * 15,
        out_specs=(anywhere,) * 4,
        scratch_shapes=[
            pltpu.VMEM(latents.shape, F32),
            pltpu.VMEM(senders.shape, jnp.int32),
            pltpu.VMEM(senders.shape, jnp.int32),
            pltpu.VMEM(send_rows.shape[1:], jnp.int32),
        ] + [pltpu.VMEM(edge_gain.shape, F32)] * 6 + [
            pltpu.VMEM((nodes, width), F32),
            pltpu.VMEM((shards * slot, width), BF16),
            pltpu.VMEM((edges, LANES), jnp.int32),
            pltpu.VMEM((edges, LANES), jnp.int32),
            pltpu.VMEM(senders.shape, jnp.int32),
            pltpu.VMEM((edges, width), F32),
            pltpu.VMEM((edges, width), F32),
            pltpu.VMEM(edge_first_weight.shape[1:], BF16),
            pltpu.VMEM(edge_second_weight.shape[1:], BF16),
            pltpu.VMEM(node_first_weight.shape[1:], BF16),
            pltpu.VMEM(node_second_weight.shape[1:], BF16),
            pltpu.VMEM(edge_first_weight.shape[1:], BF16),
            pltpu.VMEM(latents.shape, BF16),
            pltpu.VMEM((bands, nodes, half), BF16),
            pltpu.VMEM((bands, nodes, half), F32),
            pltpu.VMEM((shards, slot, width), BF16),
            pltpu.VMEM((shards, slot, width), BF16),
            pltpu.VMEM((shards, slot, width), BF16),
            pltpu.VMEM((shards, slot, width), BF16),
            pltpu.VMEM((2 * nodes, width), BF16),
            pltpu.VMEM((nodes, width), F32),
            dma((16,)), dma((4,)),
            dma((bands,)), dma((bands,)), dma((bands,)), dma((bands,)),
            dma((shards,)), dma((shards,)), dma((shards,)), dma((shards,)),
        ],
        compiler_params=pltpu.CompilerParams(
            collective_id=0, has_side_effects=True, vmem_limit_bytes=67043328
        ),
        name="layer_one",
    )(
        block_counts, latents, senders, receivers, send_rows, edge_first_bias, edge_gain, edge_offset,
        node_first_bias, node_gain, node_offset,
        edge_latents, edge_first_weight, edge_second_weight, node_first_weight, node_second_weight,
    )

    def whole(array):
        return pl.BlockSpec(array.shape, lambda c: (0,) * array.ndim)

    def second(array):
        return pl.BlockSpec((1,) + array.shape[1:], lambda c: (1, 0, 0))

    def stream(columns):
        return pl.BlockSpec((chunk, columns), lambda c: (c, 0))

    indices = pl.BlockSpec((chunk // LANES, 1, LANES), lambda c: (c, 0, 0))
    return pl.pallas_call(
        functools.partial(second_kernel, chunks),
        grid=(chunks,),
        out_shape=(
            jax.ShapeDtypeStruct((nodes, width), F32),
            jax.ShapeDtypeStruct((edges, width), F32),
        ),
        in_specs=[
            scalars, stream(width), stream(width), indices, indices,
            whole(table), second(edge_second_weight), whole(edge_gain), whole(edge_offset),
            whole(node_state), second(node_first_weight), whole(node_first_bias), second(node_second_weight),
            whole(node_gain), whole(node_offset),
        ],
        out_specs=(whole(node_state), stream(width)),
        scratch_shapes=[pltpu.VMEM((nodes, width), F32)],
        compiler_params=pltpu.CompilerParams(
            dimension_semantics=("arbitrary",), vmem_limit_bytes=67043328
        ),
        name="layer_two",
    )(
        block_counts, pre, state, senders, receivers, table, edge_second_weight, edge_gain, edge_offset,
        node_state, node_first_weight, node_first_bias, node_second_weight, node_gain, node_offset,
    )


def solution(mesh):
    owned = P(("patch", "band"))
    return jax.shard_map(
        functools.partial(shards_body, mesh.shape["patch"], mesh.shape["band"]),
        mesh=mesh,
        in_specs=(P("patch", "band"), owned, owned, owned, owned, owned) + (P(),) * 10,
        out_specs=(owned, owned),
        check_vma=False,
    )
```

profile of v0, /device:TPU:0, one launch (start us, length us, event | category | flops | bytes accessed | tf_op | source)
XLA Modules:
  0.0 56.5 jit_solution(9908432114159835653)
XLA Ops:
  0.6 1.3 %reshape.10.senders_hbm.senders_ref = s32[20,1,128]{2,1,0:T(1,128)} reshape(s32[2560]{0:T(1024)} %param.18) | data formatting | bytes 20480 | tf_op jit(solution)/shard_map/reshape | solution.py:330
  1.9 1.3 %reshape.11.receivers_hbm.receivers_ref = s32[20,1,128]{2,1,0:T(1,128)} reshape(s32[2560]{0:T(1024)} %param.19) | data formatting | bytes 20480 | tf_op jit(solution)/shard_map/reshape | solution.py:331
  3.3 1.4 %copy.18.lists_hbm = s32[1,32,8]{2,1,0:T(8,128)} copy(s32[1,32,8]{1,2,0:T(8,128)} %param.21) | data formatting | bytes 2048 | tf_op args[5]
  4.6 39.2 %layer_one.1 = (f32[320,512]{1,0:T(8,128)}, bf16[256,512]{1,0:T(8,128)(2,1)}, f32[2560,512]{1,0:T(8,128)}, f32[2560,512]{1,0:T(8,128)}) custom-call(s32[20]{0:T(128)} %counts_ref.3, f32[640,256]{1,0:T(8,128)} %lat_hbm.1, s32[20,1,128]{2,1,0:T(1,128)} %reshape.10.senders_hbm.senders_ref, s32[20,1,128]{2,1,0:T(1,128)} %reshape.11.receivers_hbm.receivers_ref, ...), custom_call_target="tpu_custom_call" | custom-call | tf_op jit(solution)/shard_map/layer_one/pallas_call | solution.py:335
  43.8 12.7 %layer_two.1 = (f32[320,512]{1,0:T(8,128)}, f32[2560,512]{1,0:T(8,128)}) custom-call(s32[20]{0:T(128)} %counts_ref.3, f32[2560,512]{1,0:T(8,128)} %get-tuple-element.6.pre_ref, f32[2560,512]{1,0:T(8,128)} %get-tuple-element.7.state_ref, s32[20,1,128]{2,1,0:T(1,128)} %reshape.10.senders_hbm.senders_ref, s32[20,1,128]{2,1,0:T(1,128)} %reshape.11.receivers_hbm.receivers_ref, ...), custom_call_target="tpu_custom_call" | custom-call | tf_op jit(solution)/shard_map/layer_two/pallas_call | solution.py:396
where the time goes:
time: 56.9 us; the launch traced here: 56.5 us
  Pallas kernels  51.9 us (91%)
  local copies, waits for them, and re-layouts  3.99 us (7%)
  between operations  0.64 us (1%)
    pallas_call x1, Pallas kernels, shards_body(): pl.pallas_call(functools.partial(first_kernel, patches, bands, chunk), ou...  39.2 us
    pallas_call x1, Pallas kernels, shards_body(): pl.pallas_call(functools.partial(second_kernel, chunks), grid=(chunks,),...  12.7 us
    unnamed x1, local copies, waits for them, and re-layouts  1.37 us
    reshape x1, local copies, waits for them, and re-layouts, shards_body(): receivers = edge_receiver.reshape(edges // LANES, 1, LANES)  1.31 us
    reshape x1, local copies, waits for them, and re-layouts, shards_body(): senders = edge_sender.reshape(edges // LANES, 1, LANES)  1.31 us

commit v1 on v0

v1 whole, which is shorter than its diff:
```python
import functools

import jax
import jax.numpy as jnp
from jax import lax
from jax.experimental import pallas as pl
from jax.experimental.pallas import tpu as pltpu
from jax.sharding import PartitionSpec as P

epsilon = 1e-05
MESH = pl.DeviceIdType.MESH
F32 = jnp.float32
BF16 = jnp.bfloat16
LANES = 128


def dot(a, b):
    return jnp.dot(a, b, preferred_element_type=F32)


def layer_norm(values, gain, offset):
    centre = values - jnp.mean(values, axis=-1, keepdims=True)
    spread = jnp.mean(centre * centre, axis=-1, keepdims=True)
    return centre * lax.rsqrt(spread + epsilon) * gain + offset


def swish(v):
    h = 0.5 * v
    return (h * jnp.tanh(h) + h).astype(BF16)


def lanes_hot(column_sets):
    pieces = []
    lane = lax.broadcasted_iota(jnp.int32, (LANES, LANES), 1)
    for group, columns in enumerate(column_sets):
        places = lane + group * LANES
        hit = places == columns[0]
        for other in columns[1:]:
            hit = hit | (places == other)
        pieces.append(jnp.where(hit, 1.0, 0.0).astype(BF16))
    return jnp.concatenate(pieces, axis=1)


def rows_hot(row, height):
    places = lax.broadcasted_iota(jnp.int32, (height, row.shape[1]), 0)
    return jnp.where(places == row, 1.0, 0.0).astype(BF16)


def lists_hot(lists, nodes):
    slots, shards = lists.shape
    rows = shards * slots
    row_place = lax.broadcasted_iota(jnp.int32, (rows, shards), 0)
    shard_place = lax.broadcasted_iota(jnp.int32, (rows, shards), 1)
    spread = jnp.where(lax.div(row_place, slots) == shard_place, 1.0, 0.0).astype(BF16)
    contract = (((1,), (1,)), ((), ()))

    def over(part):
        return lax.dot_general(spread, part.astype(F32).astype(BF16), contract, preferred_element_type=F32)

    picked = over(jnp.right_shift(lists, 4)) * 16.0 + over(jnp.bitwise_and(lists, 15))
    place = lax.rem(lax.broadcasted_iota(jnp.int32, picked.shape, 0), slots)
    slot_place = lax.broadcasted_iota(jnp.int32, picked.shape, 1)
    wanted = jnp.sum(jnp.where(place == slot_place, picked, 0.0), axis=1, keepdims=True)
    node_place = lax.broadcasted_iota(jnp.int32, (rows, nodes), 1).astype(F32)
    return jnp.where(node_place == wanted, 1.0, 0.0).astype(BF16)


def finish(
    chunks, chunk, counts_ref, pre, halo_hot, halo_table, second, gain, offset,
    state, low, low_row, scatter_hot, hidden, summed, emit,
):
    blocks = chunk // LANES
    places = lax.broadcasted_iota(jnp.int32, (LANES, state.shape[1]), 0)

    def part(c):
        return pl.ds(c * chunk, chunk)

    def gather(c):
        hidden[c % 2] = swish(dot(halo_hot[part(c), :], halo_table) + pre[part(c), :])

    def renew(c):
        update = layer_norm(dot(hidden[c % 2], second), gain, offset)
        for i in range(blocks):
            here = pl.ds(c * chunk + i * LANES, LANES)
            kept = jnp.where(places < counts_ref[c * blocks + i], update[i * LANES : (i + 1) * LANES], 0.0)
            fresh = state[here, :] + kept
            low[pl.ds(low_row(c) + i * LANES, LANES), :] = fresh.astype(BF16)
            emit(here, fresh)

    def scatter(c):
        added = dot(scatter_hot[:, part(c)], low[pl.ds(low_row(c), chunk), :])
        summed[...] = added if c == 0 else summed[...] + added

    for step in range(chunks + 2):
        if 1 <= step <= chunks:
            renew(step - 1)
        if step < chunks:
            gather(step)
        if step >= 2:
            scatter(step - 2)


def node_step(node_pre, summed, first, second, gain, offset):
    v = node_pre + dot(summed.astype(BF16), first)
    return layer_norm(dot(swish(v), second), gain, offset)


def first_kernel(
    patches, bands, chunk,
    counts_hbm, lat_hbm, senders_hbm, receivers_hbm, lists_hbm, eb_hbm, eg_hbm, eo_hbm, nb_hbm, ng_hbm, no_hbm,
    edge_hbm, ew1_hbm, ew2_hbm, nw1_hbm, nw2_hbm,
    state, pre, halo_hot, scatter_hot, table_out, node_out, node_pre, w2_out, v1_out, v2_out,
    counts_ref, lat_ref, senders_ref, receivers_ref, lists_in, eb_ref, eg_ref, eo_ref, nb_ref, ng_ref, no_ref,
    w1, w2, v1, v2, x1, own_lists, node_hot, table, low, hidden, low_out, rest_out, low_in, rest_in,
    out_a, in_a, out_b, in_b, summed,
    load_sem, list_send, list_recv, low_send, low_recv, rest_send, rest_recv, send_a, recv_a, send_b, recv_b,
):
    shards = patches * bands
    patch, band = lax.axis_index("patch"), lax.axis_index("band")
    me = patch * bands + band
    nodes = node_out.shape[0]
    edges, width = state.shape
    half = lat_ref.shape[1]
    chunks = edges // chunk
    blocks = edges // LANES
    slot = out_b.shape[1]

    loads = [
        pltpu.make_async_copy(src, dst, load_sem.at[i])
        for i, (src, dst) in enumerate((
            (lists_hbm.at[0], lists_in.at[band]), (lat_hbm, lat_ref), (counts_hbm, counts_ref),
            (senders_hbm, senders_ref), (receivers_hbm, receivers_ref),
            (edge_hbm, state), (ew1_hbm.at[0], w1), (eb_hbm, eb_ref),
            (ew2_hbm.at[0], w2), (nw1_hbm.at[0], v1), (nw2_hbm.at[0], v2),
            (eg_hbm, eg_ref), (eo_hbm, eo_ref), (nb_hbm, nb_ref), (ng_hbm, ng_ref), (no_hbm, no_ref),
            (ew1_hbm.at[1], x1), (ew2_hbm.at[1], w2_out),
            (nw1_hbm.at[1], v1_out), (nw2_hbm.at[1], v2_out),
        ))
    ]
    for load in loads:
        load.start()

    def place(q):
        return (lax.div(q, bands), lax.rem(q, bands))

    barrier = pltpu.get_barrier_semaphore()
    for i in range(1, bands):
        pl.semaphore_signal(barrier, inc=1, device_id=(patch, lax.rem(band + i, bands)), device_id_type=MESH)

    def greet(i, c):
        other = lax.rem(patch + i, patches)
        for j in range(bands):
            pl.semaphore_signal(barrier, inc=1, device_id=(other, j), device_id_type=MESH)
        return c

    lax.fori_loop(1, patches, greet, 0)
    loads[0].wait()
    loads[1].wait()
    for c in range(bands):
        rows = lat_ref[c * nodes : (c + 1) * nodes, :]
        low_out[c] = rows.astype(BF16)
        rest_out[c] = (rows - low_out[c].astype(F32)).astype(BF16)
    low_in[band] = low_out[band]
    rest_in[band] = rest_out[band]
    pl.semaphore_wait(barrier, shards - 1)

    def exchange(source, target, ss, rs):
        return [
            pltpu.make_async_remote_copy(
                src_ref=source(lax.rem(band + i, bands)), dst_ref=target, send_sem=ss.at[i], recv_sem=rs.at[i],
                device_id=(patch, lax.rem(band + i, bands)), device_id_type=MESH,
            )
            for i in range(1, bands)
        ]

    list_copies = exchange(lambda other: lists_in.at[band], lists_in.at[band], list_send, list_recv)
    low_copies = exchange(lambda other: low_out.at[other], low_in.at[band], low_send, low_recv)
    rest_copies = exchange(lambda other: rest_out.at[other], rest_in.at[band], rest_send, rest_recv)
    for copy in list_copies:
        copy.start()

    def to_all(source, target, ss, rs):
        def go(k, c):
            q = lax.rem(me + k, shards)
            pltpu.make_async_remote_copy(
                src_ref=source.at[q], dst_ref=target, send_sem=ss, recv_sem=rs,
                device_id=place(q), device_id_type=MESH,
            ).start()
            return c

        lax.fori_loop(1, shards, go, 0)

    def from_all(source, target, ss, rs):
        others = pl.ds(0, shards - 1)
        pltpu.make_async_remote_copy(
            src_ref=source.at[others], dst_ref=target.at[others], send_sem=ss, recv_sem=rs,
            device_id=(patch, lax.rem(band + 1, bands)), device_id_type=MESH,
        ).wait()

    def send_band(i):
        owner = lax.rem(band + i, bands)
        hot = lists_hot(lists_in[owner], nodes)
        if i == 0:
            own_lists[...] = hot
        sender = patch * bands + owner
        out_a[i] = dot(hot, low_out[owner]).reshape(shards, slot, half).astype(BF16)
        in_a[band, sender] = out_a[i, me]
        to_all(out_a.at[i], in_a.at[band, sender], send_a.at[i], recv_a.at[i])

    send_band(0)
    for copy in low_copies:
        copy.start()
    for i in range(1, bands):
        list_copies[i - 1].wait()
        send_band(i)
    for copy in rest_copies:
        copy.start()

    def part(c):
        return pl.ds(pl.multiple_of(c * chunk, chunk), chunk)

    for load in loads[2:8]:
        load.wait()

    def own_edges(c, carry):
        pre[part(c), :] = dot(state[part(c), :].astype(BF16), w1[0:width, :]) + eb_ref[0:1, :]
        return carry

    lax.fori_loop(0, chunks, own_edges, 0)

    def columns_of(ref):
        rows = [ref[pl.ds(j * LANES, LANES)].reshape(1, LANES) for j in range(blocks)]
        return jnp.concatenate(rows + [jnp.zeros((LANES - blocks, LANES), jnp.int32)], axis=0).T

    sender_columns, receiver_columns = columns_of(senders_ref), columns_of(receivers_ref)
    edge_place = lax.broadcasted_iota(jnp.int32, (1, LANES), 1)
    for j in range(blocks):
        here = slice(j * LANES, (j + 1) * LANES)
        sender = jnp.broadcast_to(sender_columns[:, j : j + 1], (LANES, LANES))
        receiver = jnp.broadcast_to(receiver_columns[:, j : j + 1], (LANES, LANES)) + nodes
        local, beyond = jnp.where(sender < nodes, sender, -1), sender - nodes
        sets = []
        for first in range(0, 2 * nodes, LANES):
            sets.append([local] * (first < nodes) + [receiver] * (first + LANES > nodes))
        node_hot[here, :] = lanes_hot(sets)
        halo_hot[here, :] = lanes_hot([[beyond]] * (halo_hot.shape[1] // LANES))
        row = receivers_ref[pl.ds(j * LANES, LANES)].reshape(1, LANES)
        scatter_hot[:, here] = rows_hot(jnp.where(edge_place < counts_ref[j], row, -1), nodes)

    for copy in low_copies:
        copy.wait()
    node_low = jnp.concatenate([low_in[i] for i in range(bands)], axis=1)
    table[0:nodes, :] = dot(node_low, w1[width : 2 * width, :]).astype(BF16)
    table[nodes:, :] = dot(node_low, w1[2 * width :, :]).astype(BF16)

    def own_nodes(c, carry):
        pre[part(c), :] += dot(node_hot[part(c), :], table[...])
        return carry

    lax.fori_loop(0, chunks, own_nodes, 0)
    for load in loads[8:]:
        load.wait()
    node_pre[...] = dot(node_low, v1[0:width, :]) + nb_ref[0:1, :]
    for i in range(bands):
        from_all(out_a.at[i], in_a.at[0], send_a.at[i], recv_a.at[i])

    def flat(values):
        return values.astype(F32).reshape(shards * slot, values.shape[2]).astype(BF16)

    halo = jnp.concatenate([flat(in_a[i]) for i in range(bands)], axis=1)
    table_out[...] = dot(halo, w1[width : 2 * width, :]).astype(BF16)

    def keep(here, fresh):
        state[here, :] = fresh

    finish(
        chunks, chunk, counts_ref, pre, halo_hot, table_out[...], w2[...], eg_ref[0:1, :], eo_ref[0:1, :],
        state, low, lambda c: c * chunk, scatter_hot, hidden, summed, keep,
    )
    for copy in rest_copies:
        copy.wait()
    wide = [low_in[i].astype(F32) + rest_in[i].astype(F32) for i in range(bands)]
    node_state = jnp.concatenate(wide, axis=1) + node_step(
        node_pre[...], summed[...], v1[width:, :], v2[...], ng_ref[0:1, :], no_ref[0:1, :]
    )
    node_out[...] = node_state
    node_low = node_state.astype(BF16)
    out_b[...] = dot(own_lists[...], node_low).reshape(shards, slot, width).astype(BF16)
    in_b[me] = out_b[me]
    to_all(out_b, in_b.at[me], send_b, recv_b)
    table[0:nodes, :] = dot(node_low, x1[width : 2 * width, :]).astype(BF16)
    table[nodes:, :] = dot(node_low, x1[2 * width :, :]).astype(BF16)
    node_pre[...] = dot(node_low, v1_out[0:width, :]) + nb_ref[1:2, :]

    def begin(c, carry):
        known = jnp.concatenate([low[part(c), :], node_hot[part(c), :]], axis=1)
        pre[part(c), :] = dot(known, jnp.concatenate([x1[0:width, :], table[...]], axis=0)) + eb_ref[1:2, :]
        return carry

    lax.fori_loop(0, chunks, begin, 0)
    from_all(out_b, in_b, send_b, recv_b)
    table_out[...] = dot(flat(in_b[...]), x1[width : 2 * width, :]).astype(BF16)


def second_kernel(
    chunk,
    counts_ref, state, pre, halo_hot, scatter_hot, table_ref, node_ref, node_pre, w2, v1, v2,
    eg_ref, eo_ref, ng_ref, no_ref,
    nodes_hbm, edges_hbm,
    nodes_out, edges_out, low, hidden, summed, store_sem,
):
    edges, width = state.shape
    chunks = edges // chunk
    blocks = edges // LANES
    stores = []

    def keep(here, fresh):
        edges_out[here, :] = fresh
        store = pltpu.make_async_copy(
            edges_out.at[here], edges_hbm.at[here], store_sem.at[len(stores)]
        )
        store.start()
        stores.append(store)

    finish(
        chunks, chunk, counts_ref, pre, halo_hot, table_ref[...], w2[...], eg_ref[1:2, :], eo_ref[1:2, :],
        state, low, lambda c: c % 2 * chunk, scatter_hot, hidden, summed, keep,
    )
    nodes_out[...] = node_ref[...] + node_step(
        node_pre[...], summed[...], v1[width:, :], v2[...], ng_ref[1:2, :], no_ref[1:2, :]
    )
    last = pltpu.make_async_copy(nodes_out, nodes_hbm, store_sem.at[blocks])
    last.start()
    for store in stores + [last]:
        store.wait()


def shards_body(
    patches, bands,
    latents, edge_latents, edge_sender, edge_receiver, block_counts, send_rows,
    edge_first_weight, edge_first_bias, edge_second_weight, edge_gain, edge_offset,
    node_first_weight, node_first_bias, node_second_weight, node_gain, node_offset,
):
    shards = patches * bands
    edges, width = edge_latents.shape
    nodes = latents.shape[0] // bands
    slot = send_rows.shape[2]
    half = latents.shape[1]
    chunk = next(c for c in (512, 256, 128) if edges % c == 0)
    scalars, far = pl.BlockSpec(memory_space=pltpu.SMEM), pl.BlockSpec(memory_space=pltpu.HBM)
    near = pl.BlockSpec(memory_space=pltpu.VMEM)
    dma = pltpu.SemaphoreType.DMA

    def shaped(*shape, kind=BF16):
        return jax.ShapeDtypeStruct(shape, kind)

    def held(*shape, kind=BF16):
        return pltpu.VMEM(shape, kind)

    def afar(array):
        return pltpu.with_memory_space_constraint(array, pltpu.HBM)

    handed = pl.pallas_call(
        functools.partial(first_kernel, patches, bands, chunk),
        out_shape=(
            held(edges, width, kind=F32),
            held(edges, width, kind=F32),
            held(edges, shards * slot),
            held(nodes, edges),
            held(shards * slot, width),
            held(nodes, width, kind=F32),
            held(nodes, width, kind=F32),
            held(*edge_second_weight.shape[1:]),
            held(*node_first_weight.shape[1:]),
            held(*node_second_weight.shape[1:]),
        ),
        in_specs=[far] * 16,
        out_specs=(near,) * 10,
        scratch_shapes=[
            pltpu.SMEM(block_counts.shape, jnp.int32),
            pltpu.VMEM(latents.shape, F32),
            pltpu.VMEM((edges,), jnp.int32),
            pltpu.VMEM((edges,), jnp.int32),
            pltpu.VMEM((bands, slot, shards), jnp.int32),
        ] + [pltpu.VMEM(edge_gain.shape, F32)] * 6 + [
            pltpu.VMEM(edge_first_weight.shape[1:], BF16),
            pltpu.VMEM(edge_second_weight.shape[1:], BF16),
            pltpu.VMEM(node_first_weight.shape[1:], BF16),
            pltpu.VMEM(node_second_weight.shape[1:], BF16),
            pltpu.VMEM(edge_first_weight.shape[1:], BF16),
            pltpu.VMEM((shards * slot, nodes), BF16),
            pltpu.VMEM((edges, 2 * nodes), BF16),
            pltpu.VMEM((2 * nodes, width), BF16),
            pltpu.VMEM((edges, width), BF16),
            pltpu.VMEM((2, chunk, width), BF16),
        ] + [pltpu.VMEM((bands, nodes, half), BF16)] * 4 + [
            pltpu.VMEM((bands, shards, slot, half), BF16),
            pltpu.VMEM((bands, shards, slot, half), BF16),
            pltpu.VMEM((shards, slot, width), BF16),
            pltpu.VMEM((shards, slot, width), BF16),
            pltpu.VMEM((nodes, width), F32),
            dma((20,)),
            dma((bands,)), dma((bands,)), dma((bands,)), dma((bands,)), dma((bands,)), dma((bands,)),
            dma((bands,)), dma((bands,)), dma, dma,
        ],
        compiler_params=pltpu.CompilerParams(
            collective_id=0, has_side_effects=True, vmem_limit_bytes=36 * 2**20
        ),
        name="layer_one",
    )(
        *map(afar, (
            block_counts, latents, edge_sender, edge_receiver, send_rows.transpose(0, 2, 1),
            edge_first_bias, edge_gain, edge_offset, node_first_bias, node_gain, node_offset,
            edge_latents, edge_first_weight, edge_second_weight, node_first_weight, node_second_weight,
        )),
    )
    return pl.pallas_call(
        functools.partial(second_kernel, chunk),
        out_shape=(shaped(nodes, width, kind=F32), shaped(edges, width, kind=F32)),
        in_specs=[scalars] + [near] * 14,
        out_specs=(far, far),
        scratch_shapes=[
            pltpu.VMEM((nodes, width), F32),
            pltpu.VMEM((edges, width), F32),
            pltpu.VMEM((2 * chunk, width), BF16),
            pltpu.VMEM((2, chunk, width), BF16),
            pltpu.VMEM((nodes, width), F32),
            dma((edges // LANES + 1,)),
        ],
        compiler_params=pltpu.CompilerParams(vmem_limit_bytes=24 * 2**20),
        name="layer_two",
    )(block_counts, *handed, edge_gain, edge_offset, node_gain, node_offset)


def solution(mesh):
    owned = P(("patch", "band"))
    return jax.shard_map(
        functools.partial(shards_body, mesh.shape["patch"], mesh.shape["band"]),
        mesh=mesh,
        in_specs=(P("patch", "band"), owned, owned, owned, owned, owned) + (P(),) * 10,
        out_specs=(owned, owned),
        check_vma=False,
    )
```

time: 56.9 us -> 40 us (0.70)
  Pallas kernels: 51.9 us -> 38.9 us
  local copies, waits for them, and re-layouts: 3.99 us -> 0.02 us
    pallas_call x1, Pallas kernels: 39.2 us -> 31.5 us  [shards_body(): pl.pallas_call(functools.partial(first_kernel, patches, bands, chunk), ou...]
    pallas_call x1, Pallas kernels: 12.7 us -> 7.36 us  [shards_body(): pl.pallas_call(functools.partial(second_kernel, chunk), out_shape=(shaped...]
    reshape x2 -> x0, local copies, waits for them, and re-layouts: 2.62 us -> none  [the longest x1 1.31 us: shards_body(): receivers = edge_receiver.reshape(edges // LANES, 1, LANES)]
    unnamed x1 -> x10, local copies, waits for them, and re-layouts: 1.37 us -> 0.02 us
where the time goes in v1:
time: 40 us; the launch traced here: 39.8 us
  Pallas kernels  38.9 us (97%)
  between operations  0.88 us (2%)
    pallas_call x1, Pallas kernels, shards_body(): pl.pallas_call(functools.partial(first_kernel, patches, bands, chunk), ou...  31.5 us
    pallas_call x1, Pallas kernels, shards_body(): pl.pallas_call(functools.partial(second_kernel, chunk), out_shape=(shaped...  7.36 us

profile of v1, /device:TPU:0, one launch (start us, length us, event | category | flops | bytes accessed | tf_op | source)
XLA Modules:
  0.0 39.8 jit_solution(17332272675920379695)
XLA Ops:
  0.6 0.0 copy-start
  0.6 0.0 copy-start.1
  0.7 0.0 copy-start.2
  0.7 0.0 copy-start.3
  0.7 0.0 copy-start.4
  0.7 31.5 %layer_one.1 = (f32[2560,512]{1,0:T(8,128)S(1)}, f32[2560,512]{1,0:T(8,128)S(1)}, bf16[2560,256]{1,0:T(8,128)(2,1)S(1)}, bf16[320,2560]{1,0:T(8,128)(2,1)S(1)}, ...) custom-call(s32[20]{0:T(128)} %counts_ref.1, ...), custom_call_target="tpu_custom_call" | custom-call | tf_op jit(solution)/shard_map/layer_one/pallas_call | solution.py:363
  32.2 0.0 copy-done
  32.2 0.0 copy-done.1
  32.3 0.0 copy-done.2
  32.3 0.0 copy-done.3
  32.3 0.0 copy-done.4
  32.3 7.4 %layer_two.1 = (f32[320,512]{1,0:T(8,128)}, f32[2560,512]{1,0:T(8,128)}) custom-call(s32[20]{0:T(128)S(1)} %copy-done.4, f32[2560,512]{1,0:T(8,128)S(1)} %get-tuple-element.12.state, f32[2560,512]{1,0:T(8,128)S(1)} %get-tuple-element.13.pre, bf16[2560,256]{1,0:T(8,128)(2,1)S(1)} %get-tuple-element.14.halo_hot, ...), custom_call_target="tpu_custom_call" | custom-call | tf_op jit(solution)/shard_map/layer_two/pallas_call | solution.py:417
Async XLA Ops:
  0.6 31.6 %copy-start = (f32[2,512]{1,0:T(2,128)S(1)}, f32[2,512]{1,0:T(2,128)}, u32[]{:S(2)}) copy-start(f32[2,512]{1,0:T(2,128)} %eg_ref.1) | copy-start | bytes 12292
  0.6 31.6 %copy-start.1 = (f32[2,512]{1,0:T(2,128)S(1)}, f32[2,512]{1,0:T(2,128)}, u32[]{:S(2)}) copy-start(f32[2,512]{1,0:T(2,128)} %eo_ref.1) | copy-start | bytes 12292
  0.7 31.6 %copy-start.2 = (f32[2,512]{1,0:T(2,128)S(1)}, f32[2,512]{1,0:T(2,128)}, u32[]{:S(2)}) copy-start(f32[2,512]{1,0:T(2,128)} %ng_ref.1) | copy-start | bytes 12292
  0.7 31.6 %copy-start.3 = (f32[2,512]{1,0:T(2,128)S(1)}, f32[2,512]{1,0:T(2,128)}, u32[]{:S(2)}) copy-start(f32[2,512]{1,0:T(2,128)} %no_ref.1) | copy-start | bytes 12292
  0.7 31.6 %copy-start.4 = (s32[20]{0:T(128)S(1)}, s32[20]{0:T(128)}, u32[]{:S(2)}) copy-start(s32[20]{0:T(128)} %counts_ref.1) | copy-start | bytes 244

commit v2 on v1

--- a/solution.py
+++ b/solution.py
@@ -24,53 +24,40 @@
     return centre * lax.rsqrt(spread + epsilon) * gain + offset
 
 
-def swish(v):
-    h = 0.5 * v
+def swish(h):
     return (h * jnp.tanh(h) + h).astype(BF16)
 
 
-def lanes_hot(column_sets):
-    pieces = []
-    lane = lax.broadcasted_iota(jnp.int32, (LANES, LANES), 1)
-    for group, columns in enumerate(column_sets):
-        places = lane + group * LANES
-        hit = places == columns[0]
-        for other in columns[1:]:
-            hit = hit | (places == other)
-        pieces.append(jnp.where(hit, 1.0, 0.0).astype(BF16))
-    return jnp.concatenate(pieces, axis=1)
-
-
-def rows_hot(row, height):
-    places = lax.broadcasted_iota(jnp.int32, (height, row.shape[1]), 0)
-    return jnp.where(places == row, 1.0, 0.0).astype(BF16)
+def pair_of(index):
+    low, high = jnp.bitwise_and(index, LANES - 1), jnp.right_shift(index, 7)
+    return low.astype(F32).astype(BF16), high.astype(F32).astype(BF16)
+
+
+def spread(pair, column):
+    return [jnp.broadcast_to(part[:, column : column + 1], (LANES, LANES)) for part in pair]
+
+
+def groups_hot(low, high, places, groups):
+    one, none = jnp.ones(places.shape, BF16), jnp.zeros(places.shape, BF16)
+    base = jnp.where(low == places, one, none)
+    return [jnp.where(high == jnp.full(places.shape, g, BF16), base, none) for g in groups]
 
 
 def lists_hot(lists, nodes):
     slots, shards = lists.shape
-    rows = shards * slots
-    row_place = lax.broadcasted_iota(jnp.int32, (rows, shards), 0)
-    shard_place = lax.broadcasted_iota(jnp.int32, (rows, shards), 1)
-    spread = jnp.where(lax.div(row_place, slots) == shard_place, 1.0, 0.0).astype(BF16)
-    contract = (((1,), (1,)), ((), ()))
-
-    def over(part):
-        return lax.dot_general(spread, part.astype(F32).astype(BF16), contract, preferred_element_type=F32)
-
-    picked = over(jnp.right_shift(lists, 4)) * 16.0 + over(jnp.bitwise_and(lists, 15))
-    place = lax.rem(lax.broadcasted_iota(jnp.int32, picked.shape, 0), slots)
-    slot_place = lax.broadcasted_iota(jnp.int32, picked.shape, 1)
-    wanted = jnp.sum(jnp.where(place == slot_place, picked, 0.0), axis=1, keepdims=True)
-    node_place = lax.broadcasted_iota(jnp.int32, (rows, nodes), 1).astype(F32)
-    return jnp.where(node_place == wanted, 1.0, 0.0).astype(BF16)
+    place = lax.broadcasted_iota(jnp.int32, (slots, nodes), 1)
+    rows = [
+        jnp.where(place == jnp.broadcast_to(lists[:, q : q + 1], (slots, nodes)), 1.0, 0.0) for q in range(shards)
+    ]
+    return jnp.concatenate(rows, axis=0).astype(BF16)
 
 
 def finish(
-    chunks, chunk, counts_ref, pre, halo_hot, halo_table, second, gain, offset,
-    state, low, low_row, scatter_hot, hidden, summed, emit,
+    chunks, chunk, counts_ref, pre, halo_hot, halo_table, second, gain,
+    base, low, low_row, scatter_hot, hidden, summed, emit,
 ):
     blocks = chunk // LANES
-    places = lax.broadcasted_iota(jnp.int32, (LANES, state.shape[1]), 0)
+    places = lax.broadcasted_iota(jnp.int32, (LANES, 1), 0)
 
     def part(c):
         return pl.ds(c * chunk, chunk)
@@ -79,11 +66,13 @@
         hidden[c % 2] = swish(dot(halo_hot[part(c), :], halo_table) + pre[part(c), :])
 
     def renew(c):
-        update = layer_norm(dot(hidden[c % 2], second), gain, offset)
+        values = dot(hidden[c % 2], second)
+        centre = values - jnp.mean(values, axis=-1, keepdims=True)
+        scale = lax.rsqrt(jnp.mean(centre * centre, axis=-1, keepdims=True) + epsilon)
         for i in range(blocks):
-            here = pl.ds(c * chunk + i * LANES, LANES)
-            kept = jnp.where(places < counts_ref[c * blocks + i], update[i * LANES : (i + 1) * LANES], 0.0)
-            fresh = state[here, :] + kept
+            here, rows = pl.ds(c * chunk + i * LANES, LANES), slice(i * LANES, (i + 1) * LANES)
+            kept = jnp.where(places < counts_ref[c * blocks + i], scale[rows], 0.0)
+            fresh = base[here, :] + centre[rows] * kept * gain
             low[pl.ds(low_row(c) + i * LANES, LANES), :] = fresh.astype(BF16)
             emit(here, fresh)
 
@@ -101,8 +90,17 @@
 
 
 def node_step(node_pre, summed, first, second, gain, offset):
-    v = node_pre + dot(summed.astype(BF16), first)
-    return layer_norm(dot(swish(v), second), gain, offset)
+    h = node_pre + 0.5 * dot(summed.astype(BF16), first)
+    return layer_norm(dot(swish(h), second), gain, offset)
+
+
+def with_offset(state, counts_ref, first, offset):
+    places = lax.broadcasted_iota(jnp.int32, (LANES, 1), 0)
+    pieces = []
+    for i in range(state.shape[0] // LANES):
+        usable = places < counts_ref[first + i]
+        pieces.append(state[i * LANES : (i + 1) * LANES] + jnp.where(usable, offset, 0.0))
+    return jnp.concatenate(pieces, axis=0)
 
 
 def first_kernel(
@@ -162,6 +160,16 @@
         rest_out[c] = (rows - low_out[c].astype(F32)).astype(BF16)
     low_in[band] = low_out[band]
     rest_in[band] = rest_out[band]
+
+    def pick_band(i):
+        owner = lax.rem(band + i, bands)
+        hot = lists_hot(lists_in[owner], nodes)
+        if i == 0:
+            own_lists[...] = hot
+        out_a[i] = dot(hot, low_out[owner]).reshape(shards, slot, half).astype(BF16)
+        in_a[band, patch * bands + owner] = out_a[i, me]
+
+    pick_band(0)
     pl.semaphore_wait(barrier, shards - 1)
 
     def exchange(source, target, ss, rs):
@@ -198,69 +206,73 @@
         ).wait()
 
     def send_band(i):
-        owner = lax.rem(band + i, bands)
-        hot = lists_hot(lists_in[owner], nodes)
-        if i == 0:
-            own_lists[...] = hot
-        sender = patch * bands + owner
-        out_a[i] = dot(hot, low_out[owner]).reshape(shards, slot, half).astype(BF16)
-        in_a[band, sender] = out_a[i, me]
+        sender = patch * bands + lax.rem(band + i, bands)
         to_all(out_a.at[i], in_a.at[band, sender], send_a.at[i], recv_a.at[i])
 
-    send_band(0)
     for copy in low_copies:
         copy.start()
+    send_band(0)
+
+    def part(c):
+        return slice(c * chunk, (c + 1) * chunk)
+
+    for load in loads[2:8]:
+        load.wait()
+
+    def matrix_of(ref):
+        rows = [ref[pl.ds(j * LANES, LANES)].reshape(1, LANES) for j in range(blocks)]
+        return jnp.concatenate(rows + [jnp.zeros((LANES - blocks, LANES), jnp.int32)], axis=0)
+
+    senders, receivers = matrix_of(senders_ref).T, matrix_of(receivers_ref).T
+    local_pair = pair_of(jnp.where(senders < nodes, senders, -1))
+    halo_pair = pair_of(senders - nodes)
+    receiver_pair = pair_of(receivers + nodes)
+    lane = lax.broadcasted_iota(jnp.int32, (LANES, LANES), 1).astype(F32).astype(BF16)
+    row_place = lax.broadcasted_iota(jnp.int32, (LANES, LANES), 0).astype(F32).astype(BF16)
+    edge_place = lax.broadcasted_iota(jnp.int32, (1, LANES), 1)
+    first_receiver, node_groups = nodes // LANES, 2 * nodes // LANES
+    last_local = (nodes - 1) // LANES
+
+    def build_hot(j):
+        here = slice(j * LANES, (j + 1) * LANES)
+        local = groups_hot(*spread(local_pair, j), lane, range(last_local + 1))
+        entering = groups_hot(*spread(receiver_pair, j), lane, range(first_receiver, node_groups))
+        for g in range(node_groups):
+            shown = [x for x in (
+                local[g] if g <= last_local else None, entering[g - first_receiver] if g >= first_receiver else None
+            ) if x is not None]
+            node_hot[here, g * LANES : (g + 1) * LANES] = sum(shown[1:], shown[0])
+        beyond = groups_hot(*spread(halo_pair, j), lane, range(halo_hot.shape[1] // LANES))
+        halo_hot[here, :] = jnp.concatenate(beyond, axis=1)
+        row = jnp.where(edge_place < counts_ref[j], receivers_ref[pl.ds(j * LANES, LANES)].reshape(1, LANES), -1)
+        low_row, high_row = [jnp.broadcast_to(x, (LANES, LANES)) for x in pair_of(row)]
+        for g, hot in enumerate(groups_hot(low_row, high_row, row_place, range(last_local + 1))):
+            rows = min(LANES, nodes - g * LANES)
+            scatter_hot[g * LANES : g * LANES + rows, here] = hot[0:rows]
+
+    for c in range(chunks):
+        pre[part(c), :] = dot(state[part(c), :].astype(BF16), w1[0:width, :]) + eb_ref[0:1, :]
+        for j in range(c * chunk // LANES, (c + 1) * chunk // LANES):
+            build_hot(j)
+
     for i in range(1, bands):
         list_copies[i - 1].wait()
+        pick_band(i)
         send_band(i)
+    for copy in low_copies:
+        copy.wait()
     for copy in rest_copies:
         copy.start()
-
-    def part(c):
-        return pl.ds(pl.multiple_of(c * chunk, chunk), chunk)
-
-    for load in loads[2:8]:
-        load.wait()
-
-    def own_edges(c, carry):
-        pre[part(c), :] = dot(state[part(c), :].astype(BF16), w1[0:width, :]) + eb_ref[0:1, :]
-        return carry
-
-    lax.fori_loop(0, chunks, own_edges, 0)
-
-    def columns_of(ref):
-        rows = [ref[pl.ds(j * LANES, LANES)].reshape(1, LANES) for j in range(blocks)]
-        return jnp.concatenate(rows + [jnp.zeros((LANES - blocks, LANES), jnp.int32)], axis=0).T
-
-    sender_columns, receiver_columns = columns_of(senders_ref), columns_of(receivers_ref)
-    edge_place = lax.broadcasted_iota(jnp.int32, (1, LANES), 1)
-    for j in range(blocks):
-        here = slice(j * LANES, (j + 1) * LANES)
-        sender = jnp.broadcast_to(sender_columns[:, j : j + 1], (LANES, LANES))
-        receiver = jnp.broadcast_to(receiver_columns[:, j : j + 1], (LANES, LANES)) + nodes
-        local, beyond = jnp.where(sender < nodes, sender, -1), sender - nodes
-        sets = []
-        for first in range(0, 2 * nodes, LANES):
-            sets.append([local] * (first < nodes) + [receiver] * (first + LANES > nodes))
-        node_hot[here, :] = lanes_hot(sets)
-        halo_hot[here, :] = lanes_hot([[beyond]] * (halo_hot.shape[1] // LANES))
-        row = receivers_ref[pl.ds(j * LANES, LANES)].reshape(1, LANES)
-        scatter_hot[:, here] = rows_hot(jnp.where(edge_place < counts_ref[j], row, -1), nodes)
-
-    for copy in low_copies:
-        copy.wait()
     node_low = jnp.concatenate([low_in[i] for i in range(bands)], axis=1)
     table[0:nodes, :] = dot(node_low, w1[width : 2 * width, :]).astype(BF16)
     table[nodes:, :] = dot(node_low, w1[2 * width :, :]).astype(BF16)
 
-    def own_nodes(c, carry):
-        pre[part(c), :] += dot(node_hot[part(c), :], table[...])
-        return carry
-
-    lax.fori_loop(0, chunks, own_nodes, 0)
     for load in loads[8:]:
         load.wait()
-    node_pre[...] = dot(node_low, v1[0:width, :]) + nb_ref[0:1, :]
+    for c in range(chunks):
+        pre[part(c), :] = 0.5 * (pre[part(c), :] + dot(node_hot[part(c), :], table[...]))
+        state[part(c), :] = with_offset(state[part(c), :], counts_ref, c * chunk // LANES, eo_ref[0:1, :])
+    node_pre[...] = 0.5 * (dot(node_low, v1[0:width, :]) + nb_ref[0:1, :])
     for i in range(bands):
         from_all(out_a.at[i], in_a.at[0], send_a.at[i], recv_a.at[i])
 
@@ -268,13 +280,13 @@
         return values.astype(F32).reshape(shards * slot, values.shape[2]).astype(BF16)
 
     halo = jnp.concatenate([flat(in_a[i]) for i in range(bands)], axis=1)
-    table_out[...] = dot(halo, w1[width : 2 * width, :]).astype(BF16)
+    table_out[...] = (0.5 * dot(halo, w1[width : 2 * width, :])).astype(BF16)
 
     def keep(here, fresh):
         state[here, :] = fresh
 
     finish(
-        chunks, chunk, counts_ref, pre, halo_hot, table_out[...], w2[...], eg_ref[0:1, :], eo_ref[0:1, :],
+        chunks, chunk, counts_ref, pre, halo_hot, table_out[...], w2[...], eg_ref[0:1, :],
         state, low, lambda c: c * chunk, scatter_hot, hidden, summed, keep,
     )
     for copy in rest_copies:
@@ -290,22 +302,20 @@
     to_all(out_b, in_b.at[me], send_b, recv_b)
     table[0:nodes, :] = dot(node_low, x1[width : 2 * width, :]).astype(BF16)
     table[nodes:, :] = dot(node_low, x1[2 * width :, :]).astype(BF16)
-    node_pre[...] = dot(node_low, v1_out[0:width, :]) + nb_ref[1:2, :]
-
-    def begin(c, carry):
+    node_pre[...] = 0.5 * (dot(node_low, v1_out[0:width, :]) + nb_ref[1:2, :])
+    known_weight = jnp.concatenate([x1[0:width, :], table[...]], axis=0)
+    for c in range(chunks):
         known = jnp.concatenate([low[part(c), :], node_hot[part(c), :]], axis=1)
-        pre[part(c), :] = dot(known, jnp.concatenate([x1[0:width, :], table[...]], axis=0)) + eb_ref[1:2, :]
-        return carry
-
-    lax.fori_loop(0, chunks, begin, 0)
+        pre[part(c), :] = 0.5 * (dot(known, known_weight) + eb_ref[1:2, :])
+        state[part(c), :] = with_offset(state[part(c), :], counts_ref, c * chunk // LANES, eo_ref[1:2, :])
     from_all(out_b, in_b, send_b, recv_b)
-    table_out[...] = dot(flat(in_b[...]), x1[width : 2 * width, :]).astype(BF16)
+    table_out[...] = (0.5 * dot(flat(in_b[...]), x1[width : 2 * width, :])).astype(BF16)
 
 
 def second_kernel(
     chunk,
     counts_ref, state, pre, halo_hot, scatter_hot, table_ref, node_ref, node_pre, w2, v1, v2,
-    eg_ref, eo_ref, ng_ref, no_ref,
+    eg_ref, ng_ref, no_ref,
     nodes_hbm, edges_hbm,
     nodes_out, edges_out, low, hidden, summed, store_sem,
 ):
@@ -323,7 +333,7 @@
         stores.append(store)
 
     finish(
-        chunks, chunk, counts_ref, pre, halo_hot, table_ref[...], w2[...], eg_ref[1:2, :], eo_ref[1:2, :],
+        chunks, chunk, counts_ref, pre, halo_hot, table_ref[...], w2[...], eg_ref[1:2, :],
         state, low, lambda c: c % 2 * chunk, scatter_hot, hidden, summed, keep,
     )
     nodes_out[...] = node_ref[...] + node_step(
@@ -417,7 +427,7 @@
     return pl.pallas_call(
         functools.partial(second_kernel, chunk),
         out_shape=(shaped(nodes, width, kind=F32), shaped(edges, width, kind=F32)),
-        in_specs=[scalars] + [near] * 14,
+        in_specs=[scalars] + [near] * 13,
         out_specs=(far, far),
         scratch_shapes=[
             pltpu.VMEM((nodes, width), F32),
@@ -429,7 +439,7 @@
         ],
         compiler_params=pltpu.CompilerParams(vmem_limit_bytes=24 * 2**20),
         name="layer_two",
-    )(block_counts, *handed, edge_gain, edge_offset, node_gain, node_offset)
+    )(block_counts, *handed, edge_gain, node_gain, node_offset)
 
 
 def solution(mesh):

time: 40 us -> 35.9 us (0.90)
  Pallas kernels: 38.9 us -> 34.9 us
    pallas_call x1, Pallas kernels: 31.5 us -> 28.7 us  [shards_body(): pl.pallas_call(functools.partial(first_kernel, patches, bands, chunk), ou...]
    pallas_call x1, Pallas kernels: 7.36 us -> 6.19 us  [shards_body(): pl.pallas_call(functools.partial(second_kernel, chunk), out_shape=(shaped...]
where the time goes in v2:
time: 35.9 us; the launch traced here: 35.8 us
  Pallas kernels  34.9 us (97%)
  between operations  0.87 us (2%)
    pallas_call x1, Pallas kernels, shards_body(): pl.pallas_call(functools.partial(first_kernel, patches, bands, chunk), ou...  28.7 us
    pallas_call x1, Pallas kernels, shards_body(): pl.pallas_call(functools.partial(second_kernel, chunk), out_shape=(shaped...  6.19 us

profile of v2, /device:TPU:0, one launch (start us, length us, event | category | flops | bytes accessed | tf_op | source)
XLA Modules:
  0.0 35.8 jit_solution(12414524143837699522)
XLA Ops:
  0.6 0.0 copy-start
  0.6 0.0 copy-start.1
  0.7 0.0 copy-start.2
  0.7 0.0 copy-start.3
  0.7 28.7 %layer_one.1 = (f32[2560,512]{1,0:T(8,128)S(1)}, f32[2560,512]{1,0:T(8,128)S(1)}, bf16[2560,256]{1,0:T(8,128)(2,1)S(1)}, bf16[320,2560]{1,0:T(8,128)(2,1)S(1)}, ...) custom-call(s32[20]{0:T(128)} %counts_ref.1, ...), custom_call_target="tpu_custom_call" | custom-call | tf_op jit(solution)/shard_map/layer_one/pallas_call | solution.py:373
  29.4 0.0 copy-done
  29.4 0.0 copy-done.1
  29.4 0.0 copy-done.2
  29.4 0.0 copy-done.3
  29.4 6.2 %layer_two.1 = (f32[320,512]{1,0:T(8,128)}, f32[2560,512]{1,0:T(8,128)}) custom-call(s32[20]{0:T(128)S(1)} %copy-done.3, f32[2560,512]{1,0:T(8,128)S(1)} %get-tuple-element.12.state, f32[2560,512]{1,0:T(8,128)S(1)} %get-tuple-element.13.pre, bf16[2560,256]{1,0:T(8,128)(2,1)S(1)} %get-tuple-element.14.halo_hot, ...), custom_call_target="tpu_custom_call" | custom-call | tf_op jit(solution)/shard_map/layer_two/pallas_call | solution.py:427
Async XLA Ops:
  0.6 28.8 %copy-start = (f32[2,512]{1,0:T(2,128)S(1)}, f32[2,512]{1,0:T(2,128)}, u32[]{:S(2)}) copy-start(f32[2,512]{1,0:T(2,128)} %eg_ref.1) | copy-start | bytes 12292
  0.6 28.8 %copy-start.1 = (f32[2,512]{1,0:T(2,128)S(1)}, f32[2,512]{1,0:T(2,128)}, u32[]{:S(2)}) copy-start(f32[2,512]{1,0:T(2,128)} %ng_ref.1) | copy-start | bytes 12292
  0.7 28.8 %copy-start.2 = (f32[2,512]{1,0:T(2,128)S(1)}, f32[2,512]{1,0:T(2,128)}, u32[]{:S(2)}) copy-start(f32[2,512]{1,0:T(2,128)} %no_ref.1) | copy-start | bytes 12292
  0.7 28.8 %copy-start.3 = (s32[20]{0:T(128)S(1)}, s32[20]{0:T(128)}, u32[]{:S(2)}) copy-start(s32[20]{0:T(128)} %counts_ref.1) | copy-start | bytes 244

commit v3 on v2

--- a/solution.py
+++ b/solution.py
@@ -18,10 +18,12 @@
     return jnp.dot(a, b, preferred_element_type=F32)
 
 
-def layer_norm(values, gain, offset):
-    centre = values - jnp.mean(values, axis=-1, keepdims=True)
-    spread = jnp.mean(centre * centre, axis=-1, keepdims=True)
-    return centre * lax.rsqrt(spread + epsilon) * gain + offset
+def centred(values):
+    return values - jnp.mean(values, axis=-1, keepdims=True)
+
+
+def inverse_spread(centre):
+    return lax.rsqrt(jnp.mean(centre * centre, axis=-1, keepdims=True) + epsilon)
 
 
 def swish(h):
@@ -53,11 +55,10 @@
 
 
 def finish(
-    chunks, chunk, counts_ref, pre, halo_hot, halo_table, second, gain,
+    chunks, chunk, usable, pre, halo_hot, halo_table, second, gain,
     base, low, low_row, scatter_hot, hidden, summed, emit,
 ):
-    blocks = chunk // LANES
-    places = lax.broadcasted_iota(jnp.int32, (LANES, 1), 0)
+    groups = base.shape[1] // LANES
 
     def part(c):
         return pl.ds(c * chunk, chunk)
@@ -66,15 +67,11 @@
         hidden[c % 2] = swish(dot(halo_hot[part(c), :], halo_table) + pre[part(c), :])
 
     def renew(c):
-        values = dot(hidden[c % 2], second)
-        centre = values - jnp.mean(values, axis=-1, keepdims=True)
-        scale = lax.rsqrt(jnp.mean(centre * centre, axis=-1, keepdims=True) + epsilon)
-        for i in range(blocks):
-            here, rows = pl.ds(c * chunk + i * LANES, LANES), slice(i * LANES, (i + 1) * LANES)
-            kept = jnp.where(places < counts_ref[c * blocks + i], scale[rows], 0.0)
-            fresh = base[here, :] + centre[rows] * kept * gain
-            low[pl.ds(low_row(c) + i * LANES, LANES), :] = fresh.astype(BF16)
-            emit(here, fresh)
+        centre = centred(dot(hidden[c % 2], second))
+        kept = inverse_spread(centre) * usable[part(c), :]
+        fresh = base[part(c), :] + centre * jnp.concatenate([kept] * groups, axis=1) * gain
+        low[pl.ds(low_row(c), chunk), :] = fresh.astype(BF16)
+        emit(part(c), fresh)
 
     def scatter(c):
         added = dot(scatter_hot[:, part(c)], low[pl.ds(low_row(c), chunk), :])
@@ -91,25 +88,21 @@
 
 def node_step(node_pre, summed, first, second, gain, offset):
     h = node_pre + 0.5 * dot(summed.astype(BF16), first)
-    return layer_norm(dot(swish(h), second), gain, offset)
-
-
-def with_offset(state, counts_ref, first, offset):
-    places = lax.broadcasted_iota(jnp.int32, (LANES, 1), 0)
-    pieces = []
-    for i in range(state.shape[0] // LANES):
-        usable = places < counts_ref[first + i]
-        pieces.append(state[i * LANES : (i + 1) * LANES] + jnp.where(usable, offset, 0.0))
-    return jnp.concatenate(pieces, axis=0)
+    centre = centred(dot(swish(h), second))
+    return centre * inverse_spread(centre) * gain + offset
+
+
+def with_offset(state, usable, offset):
+    return state + jnp.concatenate([usable] * (state.shape[1] // LANES), axis=1) * offset
 
 
 def first_kernel(
     patches, bands, chunk,
     counts_hbm, lat_hbm, senders_hbm, receivers_hbm, lists_hbm, eb_hbm, eg_hbm, eo_hbm, nb_hbm, ng_hbm, no_hbm,
     edge_hbm, ew1_hbm, ew2_hbm, nw1_hbm, nw2_hbm,
-    state, pre, halo_hot, scatter_hot, table_out, node_out, node_pre, w2_out, v1_out, v2_out,
+    state, pre, usable, halo_hot, scatter_hot, table_out, node_out, node_pre, w2_out, v1_out, v2_out,
     counts_ref, lat_ref, senders_ref, receivers_ref, lists_in, eb_ref, eg_ref, eo_ref, nb_ref, ng_ref, no_ref,
-    w1, w2, v1, v2, x1, own_lists, node_hot, table, low, hidden, low_out, rest_out, low_in, rest_in,
+    w1, w2, v1, v2, x1, own_lists, node_hot, table, partial, low, hidden, low_out, rest_out, low_in, rest_in,
     out_a, in_a, out_b, in_b, summed,
     load_sem, list_send, list_recv, low_send, low_recv, rest_send, rest_recv, send_a, recv_a, send_b, recv_b,
 ):
@@ -138,28 +131,20 @@
     for load in loads:
         load.start()
 
-    def place(q):
-        return (lax.div(q, bands), lax.rem(q, bands))
-
     barrier = pltpu.get_barrier_semaphore()
     for i in range(1, bands):
         pl.semaphore_signal(barrier, inc=1, device_id=(patch, lax.rem(band + i, bands)), device_id_type=MESH)
 
-    def greet(i, c):
+    for i in range(1, patches):
         other = lax.rem(patch + i, patches)
         for j in range(bands):
             pl.semaphore_signal(barrier, inc=1, device_id=(other, j), device_id_type=MESH)
-        return c
-
-    lax.fori_loop(1, patches, greet, 0)
     loads[0].wait()
     loads[1].wait()
     for c in range(bands):
         rows = lat_ref[c * nodes : (c + 1) * nodes, :]
         low_out[c] = rows.astype(BF16)
-        rest_out[c] = (rows - low_out[c].astype(F32)).astype(BF16)
     low_in[band] = low_out[band]
-    rest_in[band] = rest_out[band]
 
     def pick_band(i):
         owner = lax.rem(band + i, bands)
@@ -187,12 +172,25 @@
     for copy in list_copies:
         copy.start()
 
+    def to_band(shift, source, target, ss, rs):
+        other = lax.rem(band + shift, bands)
+
+        def go(k, c):
+            p = lax.rem(patch + k, patches)
+            pltpu.make_async_remote_copy(
+                src_ref=source.at[p * bands + other], dst_ref=target, send_sem=ss, recv_sem=rs,
+                device_id=(p, other), device_id_type=MESH,
+            ).start()
+            return c
+
+        lax.fori_loop(0 if shift else 1, patches, go, 0)
+
     def to_all(source, target, ss, rs):
         def go(k, c):
             q = lax.rem(me + k, shards)
             pltpu.make_async_remote_copy(
                 src_ref=source.at[q], dst_ref=target, send_sem=ss, recv_sem=rs,
-                device_id=place(q), device_id_type=MESH,
+                device_id=(lax.div(q, bands), lax.rem(q, bands)), device_id_type=MESH,
             ).start()
             return c
 
@@ -205,13 +203,13 @@
             device_id=(patch, lax.rem(band + 1, bands)), device_id_type=MESH,
         ).wait()
 
-    def send_band(i):
+    def send_band(i, shift):
         sender = patch * bands + lax.rem(band + i, bands)
-        to_all(out_a.at[i], in_a.at[band, sender], send_a.at[i], recv_a.at[i])
+        to_band(shift, out_a.at[i], in_a.at[band, sender], send_a.at[i], recv_a.at[i])
 
     for copy in low_copies:
         copy.start()
-    send_band(0)
+    send_band(0, 0)
 
     def part(c):
         return slice(c * chunk, (c + 1) * chunk)
@@ -230,11 +228,13 @@
     lane = lax.broadcasted_iota(jnp.int32, (LANES, LANES), 1).astype(F32).astype(BF16)
     row_place = lax.broadcasted_iota(jnp.int32, (LANES, LANES), 0).astype(F32).astype(BF16)
     edge_place = lax.broadcasted_iota(jnp.int32, (1, LANES), 1)
+    usable_place = lax.broadcasted_iota(jnp.int32, (LANES, LANES), 0)
     first_receiver, node_groups = nodes // LANES, 2 * nodes // LANES
     last_local = (nodes - 1) // LANES
 
     def build_hot(j):
         here = slice(j * LANES, (j + 1) * LANES)
+        usable[here, :] = jnp.where(usable_place < counts_ref[j], 1.0, 0.0)
         local = groups_hot(*spread(local_pair, j), lane, range(last_local + 1))
         entering = groups_hot(*spread(receiver_pair, j), lane, range(first_receiver, node_groups))
         for g in range(node_groups):
@@ -250,29 +250,56 @@
             rows = min(LANES, nodes - g * LANES)
             scatter_hot[g * LANES : g * LANES + rows, here] = hot[0:rows]
 
-    for c in range(chunks):
+    def own_edges(c):
         pre[part(c), :] = dot(state[part(c), :].astype(BF16), w1[0:width, :]) + eb_ref[0:1, :]
         for j in range(c * chunk // LANES, (c + 1) * chunk // LANES):
             build_hot(j)
 
+    for c in range(chunks // 2):
+        own_edges(c)
     for i in range(1, bands):
         list_copies[i - 1].wait()
         pick_band(i)
-        send_band(i)
+        send_band(i, 0)
+    for c in range(chunks // 2, chunks):
+        own_edges(c)
+    for shift in range(1, bands):
+        for i in range(bands):
+            send_band(i, shift)
+    for load in loads[8:]:
+        load.wait()
+
+    def node_products(shift):
+        which = lax.rem(band + shift, bands)
+        columns = low_in[which]
+
+        def rows(first):
+            return pl.ds(pl.multiple_of(first + which * half, half), half)
+
+        return [
+            dot(columns, weight[rows(first), :]) for weight, first in ((w1, width), (w1, 2 * width), (v1, 0))
+        ]
+
+    own = node_products(0)
+    partial[0:nodes, :] = own[0]
+    partial[nodes:, :] = own[1]
+    node_pre[...] = own[2] + nb_ref[0:1, :]
+    for c in range(bands):
+        rest_out[c] = (lat_ref[c * nodes : (c + 1) * nodes, :] - low_out[c].astype(F32)).astype(BF16)
+    rest_in[band] = rest_out[band]
     for copy in low_copies:
-        copy.wait()
+        copy.wait_send()
+    for copy in low_copies:
+        copy.wait_recv()
     for copy in rest_copies:
         copy.start()
-    node_low = jnp.concatenate([low_in[i] for i in range(bands)], axis=1)
-    table[0:nodes, :] = dot(node_low, w1[width : 2 * width, :]).astype(BF16)
-    table[nodes:, :] = dot(node_low, w1[2 * width :, :]).astype(BF16)
-
-    for load in loads[8:]:
-        load.wait()
+    others = [node_products(shift) for shift in range(1, bands)]
+    table[0:nodes, :] = sum([x[0] for x in others], partial[0:nodes, :]).astype(BF16)
+    table[nodes:, :] = sum([x[1] for x in others], partial[nodes:, :]).astype(BF16)
+    node_pre[...] = 0.5 * sum([x[2] for x in others], node_pre[...])
     for c in range(chunks):
         pre[part(c), :] = 0.5 * (pre[part(c), :] + dot(node_hot[part(c), :], table[...]))
-        state[part(c), :] = with_offset(state[part(c), :], counts_ref, c * chunk // LANES, eo_ref[0:1, :])
-    node_pre[...] = 0.5 * (dot(node_low, v1[0:width, :]) + nb_ref[0:1, :])
+        state[part(c), :] = with_offset(state[part(c), :], usable[part(c), :], eo_ref[0:1, :])
     for i in range(bands):
         from_all(out_a.at[i], in_a.at[0], send_a.at[i], recv_a.at[i])
 
@@ -286,7 +313,7 @@
         state[here, :] = fresh
 
     finish(
-        chunks, chunk, counts_ref, pre, halo_hot, table_out[...], w2[...], eg_ref[0:1, :],
+        chunks, chunk, usable, pre, halo_hot, table_out[...], w2[...], eg_ref[0:1, :],
         state, low, lambda c: c * chunk, scatter_hot, hidden, summed, keep,
     )
     for copy in rest_copies:
@@ -307,21 +334,20 @@
     for c in range(chunks):
         known = jnp.concatenate([low[part(c), :], node_hot[part(c), :]], axis=1)
         pre[part(c), :] = 0.5 * (dot(known, known_weight) + eb_ref[1:2, :])
-        state[part(c), :] = with_offset(state[part(c), :], counts_ref, c * chunk // LANES, eo_ref[1:2, :])
+        state[part(c), :] = with_offset(state[part(c), :], usable[part(c), :], eo_ref[1:2, :])
     from_all(out_b, in_b, send_b, recv_b)
     table_out[...] = (0.5 * dot(flat(in_b[...]), x1[width : 2 * width, :])).astype(BF16)
 
 
 def second_kernel(
     chunk,
-    counts_ref, state, pre, halo_hot, scatter_hot, table_ref, node_ref, node_pre, w2, v1, v2,
+    state, pre, usable, halo_hot, scatter_hot, table_ref, node_ref, node_pre, w2, v1, v2,
     eg_ref, ng_ref, no_ref,
     nodes_hbm, edges_hbm,
     nodes_out, edges_out, low, hidden, summed, store_sem,
 ):
     edges, width = state.shape
     chunks = edges // chunk
-    blocks = edges // LANES
     stores = []
 
     def keep(here, fresh):
@@ -333,13 +359,13 @@
         stores.append(store)
 
     finish(
-        chunks, chunk, counts_ref, pre, halo_hot, table_ref[...], w2[...], eg_ref[1:2, :],
+        chunks, chunk, usable, pre, halo_hot, table_ref[...], w2[...], eg_ref[1:2, :],
         state, low, lambda c: c % 2 * chunk, scatter_hot, hidden, summed, keep,
     )
     nodes_out[...] = node_ref[...] + node_step(
         node_pre[...], summed[...], v1[width:, :], v2[...], ng_ref[1:2, :], no_ref[1:2, :]
     )
-    last = pltpu.make_async_copy(nodes_out, nodes_hbm, store_sem.at[blocks])
+    last = pltpu.make_async_copy(nodes_out, nodes_hbm, store_sem.at[chunks])
     last.start()
     for store in stores + [last]:
         store.wait()
@@ -357,7 +383,7 @@
     slot = send_rows.shape[2]
     half = latents.shape[1]
     chunk = next(c for c in (512, 256, 128) if edges % c == 0)
-    scalars, far = pl.BlockSpec(memory_space=pltpu.SMEM), pl.BlockSpec(memory_space=pltpu.HBM)
+    far = pl.BlockSpec(memory_space=pltpu.HBM)
     near = pl.BlockSpec(memory_space=pltpu.VMEM)
     dma = pltpu.SemaphoreType.DMA
 
@@ -375,6 +401,7 @@
         out_shape=(
             held(edges, width, kind=F32),
             held(edges, width, kind=F32),
+            held(edges, LANES, kind=F32),
             held(edges, shards * slot),
             held(nodes, edges),
             held(shards * slot, width),
@@ -385,7 +412,7 @@
             held(*node_second_weight.shape[1:]),
         ),
         in_specs=[far] * 16,
-        out_specs=(near,) * 10,
+        out_specs=(near,) * 11,
         scratch_shapes=[
             pltpu.SMEM(block_counts.shape, jnp.int32),
             pltpu.VMEM(latents.shape, F32),
@@ -401,6 +428,7 @@
             pltpu.VMEM((shards * slot, nodes), BF16),
             pltpu.VMEM((edges, 2 * nodes), BF16),
             pltpu.VMEM((2 * nodes, width), BF16),
+            pltpu.VMEM((2 * nodes, width), F32),
             pltpu.VMEM((edges, width), BF16),
             pltpu.VMEM((2, chunk, width), BF16),
         ] + [pltpu.VMEM((bands, nodes, half), BF16)] * 4 + [
@@ -427,7 +455,7 @@
     return pl.pallas_call(
         functools.partial(second_kernel, chunk),
         out_shape=(shaped(nodes, width, kind=F32), shaped(edges, width, kind=F32)),
-        in_specs=[scalars] + [near] * 13,
+        in_specs=[near] * 14,
         out_specs=(far, far),
         scratch_shapes=[
             pltpu.VMEM((nodes, width), F32),
@@ -435,11 +463,11 @@
             pltpu.VMEM((2 * chunk, width), BF16),
             pltpu.VMEM((2, chunk, width), BF16),
             pltpu.VMEM((nodes, width), F32),
-            dma((edges // LANES + 1,)),
+            dma((edges // chunk + 1,)),
         ],
         compiler_params=pltpu.CompilerParams(vmem_limit_bytes=24 * 2**20),
         name="layer_two",
-    )(block_counts, *handed, edge_gain, node_gain, node_offset)
+    )(*handed, edge_gain, node_gain, node_offset)
 
 
 def solution(mesh):

time: 35.9 us -> 34.9 us (0.972)
  the two profiles are of different devices: /device:TPU:0 before, /device:TPU:11 now
where the time goes in v3:
time: 34.9 us; the launch traced here: 34.8 us
  Pallas kernels  33.9 us (97%)
  between operations  0.85 us (2%)
    pallas_call x1, Pallas kernels, shards_body(): pl.pallas_call(functools.partial(first_kernel, patches, bands, chunk), ou...  28.3 us
    pallas_call x1, Pallas kernels, shards_body(): pl.pallas_call(functools.partial(second_kernel, chunk), out_shape=(shaped...  5.65 us

profile of v3, /device:TPU:11, one launch (start us, length us, event | category | flops | bytes accessed | tf_op | source)
XLA Modules:
  0.0 34.8 jit_solution(4994036939337770740)
XLA Ops:
  0.6 0.0 copy-start
  0.6 0.0 copy-start.1
  0.7 0.0 copy-start.2
  0.7 28.3 %layer_one.1 = (f32[2560,512]{1,0:T(8,128)S(1)}, f32[2560,512]{1,0:T(8,128)S(1)}, f32[2560,128]{1,0:T(8,128)S(1)}, bf16[2560,256]{1,0:T(8,128)(2,1)S(1)}, bf16[3...) custom-call(s32[20]{0:T(128)} %counts_hbm.1, ...), custom_call_target="tpu_custom_call" | custom-call | tf_op jit(solution)/shard_map/layer_one/pallas_call | solution.py:399
  29.0 0.0 copy-done
  29.0 0.0 copy-done.1
  29.0 0.0 copy-done.2
  29.0 5.7 %layer_two.1 = (f32[320,512]{1,0:T(8,128)}, f32[2560,512]{1,0:T(8,128)}) custom-call(f32[2560,512]{1,0:T(8,128)S(1)} %get-tuple-element.13.state, f32[2560,512]{1,0:T(8,128)S(1)} %get-tuple-element.14.pre, f32[2560,128]{1,0:T(8,128)S(1)} %get-tuple-element.15.usable, bf16[2560,256]{1,0:T(8,128)(2,1)S(1)} %get-tuple-element.16.halo_hot, ...), custom_call_target="tpu_custom_call" | custom-call | tf_op jit(solution)/shard_map/layer_two/pallas_call | solution.py:455
Async XLA Ops:
  0.6 28.3 %copy-start = (f32[2,512]{1,0:T(2,128)S(1)}, f32[2,512]{1,0:T(2,128)}, u32[]{:S(2)}) copy-start(f32[2,512]{1,0:T(2,128)} %eg_ref.1) | copy-start | bytes 12292
  0.6 28.3 %copy-start.1 = (f32[2,512]{1,0:T(2,128)S(1)}, f32[2,512]{1,0:T(2,128)}, u32[]{:S(2)}) copy-start(f32[2,512]{1,0:T(2,128)} %ng_ref.1) | copy-start | bytes 12292
  0.7 28.3 %copy-start.2 = (f32[2,512]{1,0:T(2,128)S(1)}, f32[2,512]{1,0:T(2,128)}, u32[]{:S(2)}) copy-start(f32[2,512]{1,0:T(2,128)} %no_ref.1) | copy-start | bytes 12292

commit v4 on v3

--- a/solution.py
+++ b/solution.py
@@ -80,10 +80,10 @@
     for step in range(chunks + 2):
         if 1 <= step <= chunks:
             renew(step - 1)
+        if step >= 2:
+            scatter(step - 2)
         if step < chunks:
             gather(step)
-        if step >= 2:
-            scatter(step - 2)
 
 
 def node_step(node_pre, summed, first, second, gain, offset):
@@ -175,26 +175,22 @@
     def to_band(shift, source, target, ss, rs):
         other = lax.rem(band + shift, bands)
 
-        def go(k, c):
+        for k in range(0 if shift else 1, patches):
             p = lax.rem(patch + k, patches)
             pltpu.make_async_remote_copy(
                 src_ref=source.at[p * bands + other], dst_ref=target, send_sem=ss, recv_sem=rs,
                 device_id=(p, other), device_id_type=MESH,
             ).start()
-            return c
-
-        lax.fori_loop(0 if shift else 1, patches, go, 0)
 
     def to_all(source, target, ss, rs):
-        def go(k, c):
-            q = lax.rem(me + k, shards)
-            pltpu.make_async_remote_copy(
-                src_ref=source.at[q], dst_ref=target, send_sem=ss, recv_sem=rs,
-                device_id=(lax.div(q, bands), lax.rem(q, bands)), device_id_type=MESH,
-            ).start()
-            return c
-
-        lax.fori_loop(1, shards, go, 0)
+        for k in range(patches):
+            p = lax.rem(patch + k, patches)
+            for shift in range(0 if k else 1, bands):
+                other = lax.rem(band + shift, bands)
+                pltpu.make_async_remote_copy(
+                    src_ref=source.at[p * bands + other], dst_ref=target, send_sem=ss, recv_sem=rs,
+                    device_id=(p, other), device_id_type=MESH,
+                ).start()
 
     def from_all(source, target, ss, rs):
         others = pl.ds(0, shards - 1)

time: 34.9 us -> 34.4 us (0.986)
  the two profiles are of different devices: /device:TPU:11 before, /device:TPU:0 now
where the time goes in v4:
time: 34.4 us; the launch traced here: 33.9 us
  Pallas kernels  33 us (96%)
  between operations  0.85 us (2%)
    pallas_call x1, Pallas kernels, shards_body(): pl.pallas_call(functools.partial(first_kernel, patches, bands, chunk), ou...  27.5 us
    pallas_call x1, Pallas kernels, shards_body(): pl.pallas_call(functools.partial(second_kernel, chunk), out_shape=(shaped...  5.5 us

profile of v4, /device:TPU:0, one launch (start us, length us, event | category | flops | bytes accessed | tf_op | source)
XLA Modules:
  0.0 33.9 jit_solution(7937166896707951014)
XLA Ops:
  0.6 0.0 copy-start
  0.6 0.0 copy-start.1
  0.7 0.0 copy-start.2
  0.7 27.5 %layer_one.1 = (f32[2560,512]{1,0:T(8,128)S(1)}, f32[2560,512]{1,0:T(8,128)S(1)}, f32[2560,128]{1,0:T(8,128)S(1)}, bf16[2560,256]{1,0:T(8,128)(2,1)S(1)}, bf16[3...) custom-call(s32[20]{0:T(128)} %counts_hbm.1, ...), custom_call_target="tpu_custom_call" | custom-call | tf_op jit(solution)/shard_map/layer_one/pallas_call | solution.py:395
  28.2 0.0 copy-done
  28.2 0.0 copy-done.1
  28.2 0.0 copy-done.2
  28.2 5.5 %layer_two.1 = (f32[320,512]{1,0:T(8,128)}, f32[2560,512]{1,0:T(8,128)}) custom-call(f32[2560,512]{1,0:T(8,128)S(1)} %get-tuple-element.13.state, f32[2560,512]{1,0:T(8,128)S(1)} %get-tuple-element.14.pre, f32[2560,128]{1,0:T(8,128)S(1)} %get-tuple-element.15.usable, bf16[2560,256]{1,0:T(8,128)(2,1)S(1)} %get-tuple-element.16.halo_hot, ...), custom_call_target="tpu_custom_call" | custom-call | tf_op jit(solution)/shard_map/layer_two/pallas_call | solution.py:451
Async XLA Ops:
  0.6 27.6 %copy-start = (f32[2,512]{1,0:T(2,128)S(1)}, f32[2,512]{1,0:T(2,128)}, u32[]{:S(2)}) copy-start(f32[2,512]{1,0:T(2,128)} %eg_ref.1) | copy-start | bytes 12292
  0.6 27.6 %copy-start.1 = (f32[2,512]{1,0:T(2,128)S(1)}, f32[2,512]{1,0:T(2,128)}, u32[]{:S(2)}) copy-start(f32[2,512]{1,0:T(2,128)} %ng_ref.1) | copy-start | bytes 12292
  0.7 27.6 %copy-start.2 = (f32[2,512]{1,0:T(2,128)S(1)}, f32[2,512]{1,0:T(2,128)}, u32[]{:S(2)}) copy-start(f32[2,512]{1,0:T(2,128)} %no_ref.1) | copy-start | bytes 12292
